TPU v7x, 32 devices: a whole 2x2x4 slice. The times are simulated.
32 devices in a mesh: batch: 2 (over x), row: 4 (over z), col: 4 (over y, core).
Axes of the slice: x: 2, y: 2, z: 4, core: 2. Of those that a mesh axis runs over, the one named last changes fastest.
Arguments:
- operator: bfloat16 [12288, 6144], P(('batch', 'row'), 'col'), parts along dimension 0
- start_block: float32 [12288, 256], P(('batch', 'row', 'col')), parts along dimension 0
- shifts: float32 [32], P('batch'), parts along dimension 0
Outputs:
- output 1: float32 [12288, 256], P(('batch', 'row', 'col')), parts along dimension 0
- output 2: float32 [512, 256], P('batch'), parts along dimension 0
There are 2 independent parts. A program takes and returns all parts, laid end to end along the dimension named above; each array names one.
All inputs are finite; a program needn't handle non-finite values.
Results may differ from a plain program's by a relative error of at most 0.001.
Values are sent between devices in bfloat16 or wider.
A program may use at most 1 GiB of HBM per device.

v0:
```python
import jax
import jax.numpy as jnp
from jax import lax
from jax.sharding import PartitionSpec as P

HIGHEST = lax.Precision.HIGHEST
GRID = ("row", "col")


def cholesky_solve(block, gram):
    lower = jnp.linalg.cholesky(gram)
    return lax.linalg.triangular_solve(lower, block, left_side=False, lower=True, transpose_a=True)


def solution(mesh):
    row_count = mesh.shape["row"]
    col_count = mesh.shape["col"]
    grid_size = row_count * col_count
    moves = [(index, (index % row_count) * col_count + index // row_count) for index in range(grid_size)]

    def apply_block(op_block, x_local):
        x_moved = lax.ppermute(x_local.astype(jnp.bfloat16), GRID, moves)
        x_column = lax.all_gather(x_moved, "row", axis=0, tiled=True)
        part_sum = jnp.dot(op_block, x_column, preferred_element_type=jnp.float32)
        return lax.psum_scatter(part_sum, "col", scatter_dimension=0, tiled=True)

    def orthonormalize(y_local):
        y_low = y_local.astype(jnp.bfloat16)
        gram_one = lax.psum(jnp.einsum("ka,kb->ab", y_low, y_low, preferred_element_type=jnp.float32), GRID)
        y_local = cholesky_solve(y_local, gram_one)
        gram_two = lax.psum(jnp.einsum("ka,kb->ab", y_local, y_local, precision=HIGHEST, preferred_element_type=jnp.float32), GRID)
        return cholesky_solve(y_local, gram_two)

    def local_program(op_block, x_local, shift_vals):
        for step in range(shift_vals.shape[0]):
            y_local = apply_block(op_block, x_local) - shift_vals[step] * x_local
            x_local = orthonormalize(y_local)
        image = apply_block(op_block, x_local)
        local_gram = jnp.einsum("ka,kb->ab", x_local, image, precision=HIGHEST, preferred_element_type=jnp.float32)
        return x_local, lax.psum(local_gram, GRID)

    return jax.shard_map(
        local_program,
        mesh=mesh,
        in_specs=(P(("batch", "row"), "col"), P(("batch", "row", "col"), None), P("batch")),
        out_specs=(P(("batch", "row", "col"), None), P("batch", None)),
        check_vma=False,
    )
```

profile of v0, /device:TPU:0, one launch (start us, length us, event | category | flops | bytes accessed | tf_op | source)
XLA Modules:
  0.0 6208.8 jit_solution(12155498282643259382)
XLA Ops:
  77.3 92.2 %all-reduce.35.cloned.1.call-done = f32[256,256]{0,1:T(8,128)} async-done(((f32[256,256]{0,1:T(8,128)}), f32[256,256]{0,1:T(8,128)}) %all-reduce.35.cloned.1.call-update) | async-done | bytes 262160 | tf_op jit(solution)/shard_map/psum | solution.py:29
  234.4 90.2 %all-reduce.37.cloned.1.call-done = f32[256,256]{0,1:T(8,128)} async-done(((f32[256,256]{0,1:T(8,128)}), f32[256,256]{0,1:T(8,128)}) %all-reduce.37.cloned.1.call-update) | async-done | bytes 262160 | tf_op jit(solution)/shard_map/psum | solution.py:31
  463.5 92.2 %all-reduce.39.cloned.1.call-done = f32[256,256]{0,1:T(8,128)} async-done(((f32[256,256]{0,1:T(8,128)}), f32[256,256]{0,1:T(8,128)}) %all-reduce.39.cloned.1.call-update) | async-done | bytes 262160 | tf_op jit(solution)/shard_map/psum | solution.py:29
  839.8 92.3 %all-reduce.43.cloned.1.call-done = f32[256,256]{0,1:T(8,128)} async-done(((f32[256,256]{0,1:T(8,128)}), f32[256,256]{0,1:T(8,128)}) %all-reduce.43.cloned.1.call-update) | async-done | bytes 262160 | tf_op jit(solution)/shard_map/psum | solution.py:29
  1216.2 92.3 %all-reduce.47.cloned.1.call-done = f32[256,256]{0,1:T(8,128)} async-done(((f32[256,256]{0,1:T(8,128)}), f32[256,256]{0,1:T(8,128)}) %all-reduce.47.cloned.1.call-update) | async-done | bytes 262160 | tf_op jit(solution)/shard_map/psum | solution.py:29
  1592.5 92.2 %all-reduce.51.cloned.1.call-done = f32[256,256]{0,1:T(8,128)} async-done(((f32[256,256]{0,1:T(8,128)}), f32[256,256]{0,1:T(8,128)}) %all-reduce.51.cloned.1.call-update) | async-done | bytes 262160 | tf_op jit(solution)/shard_map/psum | solution.py:29
  1750.0 90.2 %all-reduce.53.cloned.1.call-done = f32[256,256]{0,1:T(8,128)} async-done(((f32[256,256]{0,1:T(8,128)}), f32[256,256]{0,1:T(8,128)}) %all-reduce.53.cloned.1.call-update) | async-done | bytes 262160 | tf_op jit(solution)/shard_map/psum | solution.py:31
  1968.8 92.2 %all-reduce.55.cloned.1.call-done = f32[256,256]{0,1:T(8,128)} async-done(((f32[256,256]{0,1:T(8,128)}), f32[256,256]{0,1:T(8,128)}) %all-reduce.55.cloned.1.call-update) | async-done | bytes 262160 | tf_op jit(solution)/shard_map/psum | solution.py:29
  2345.0 92.1 %all-reduce.59.cloned.1.call-done = f32[256,256]{0,1:T(8,128)} async-done(((f32[256,256]{0,1:T(8,128)}), f32[256,256]{0,1:T(8,128)}) %all-reduce.59.cloned.1.call-update) | async-done | bytes 262160 | tf_op jit(solution)/shard_map/psum | solution.py:29
  2721.2 92.3 %all-reduce.63.cloned.1.call-done = f32[256,256]{0,1:T(8,128)} async-done(((f32[256,256]{0,1:T(8,128)}), f32[256,256]{0,1:T(8,128)}) %all-reduce.63.cloned.1.call-update) | async-done | bytes 262160 | tf_op jit(solution)/shard_map/psum | solution.py:29
  2878.8 90.2 %all-reduce.65.cloned.1.call-done = f32[256,256]{0,1:T(8,128)} async-done(((f32[256,256]{0,1:T(8,128)}), f32[256,256]{0,1:T(8,128)}) %all-reduce.65.cloned.1.call-update) | async-done | bytes 262160 | tf_op jit(solution)/shard_map/psum | solution.py:31
  3097.5 92.2 %all-reduce.67.cloned.1.call-done = f32[256,256]{0,1:T(8,128)} async-done(((f32[256,256]{0,1:T(8,128)}), f32[256,256]{0,1:T(8,128)}) %all-reduce.67.cloned.1.call-update) | async-done | bytes 262160 | tf_op jit(solution)/shard_map/psum | solution.py:29
  3473.8 92.3 %all-reduce.71.cloned.1.call-done = f32[256,256]{0,1:T(8,128)} async-done(((f32[256,256]{0,1:T(8,128)}), f32[256,256]{0,1:T(8,128)}) %all-reduce.71.cloned.1.call-update) | async-done | bytes 262160 | tf_op jit(solution)/shard_map/psum | solution.py:29
  3631.4 90.2 %all-reduce.73.cloned.1.call-done = f32[256,256]{0,1:T(8,128)} async-done(((f32[256,256]{0,1:T(8,128)}), f32[256,256]{0,1:T(8,128)}) %all-reduce.73.cloned.1.call-update) | async-done | bytes 262160 | tf_op jit(solution)/shard_map/psum | solution.py:31
  3850.1 92.4 %all-reduce.75.cloned.1.call-done = f32[256,256]{0,1:T(8,128)} async-done(((f32[256,256]{0,1:T(8,128)}), f32[256,256]{0,1:T(8,128)}) %all-reduce.75.cloned.1.call-update) | async-done | bytes 262160 | tf_op jit(solution)/shard_map/psum | solution.py:29
  4226.6 92.3 %all-reduce.79.cloned.1.call-done = f32[256,256]{0,1:T(8,128)} async-done(((f32[256,256]{0,1:T(8,128)}), f32[256,256]{0,1:T(8,128)}) %all-reduce.79.cloned.1.call-update) | async-done | bytes 262160 | tf_op jit(solution)/shard_map/psum | solution.py:29
  4384.2 90.2 %all-reduce.81.cloned.1.call-done = f32[256,256]{0,1:T(8,128)} async-done(((f32[256,256]{0,1:T(8,128)}), f32[256,256]{0,1:T(8,128)}) %all-reduce.81.cloned.1.call-update) | async-done | bytes 262160 | tf_op jit(solution)/shard_map/psum | solution.py:31
  4603.0 92.3 %all-reduce.83.cloned.1.call-done = f32[256,256]{0,1:T(8,128)} async-done(((f32[256,256]{0,1:T(8,128)}), f32[256,256]{0,1:T(8,128)}) %all-reduce.83.cloned.1.call-update) | async-done | bytes 262160 | tf_op jit(solution)/shard_map/psum | solution.py:29
  4979.3 92.3 %all-reduce.87.cloned.1.call-done = f32[256,256]{0,1:T(8,128)} async-done(((f32[256,256]{0,1:T(8,128)}), f32[256,256]{0,1:T(8,128)}) %all-reduce.87.cloned.1.call-update) | async-done | bytes 262160 | tf_op jit(solution)/shard_map/psum | solution.py:29
  5136.9 90.2 %all-reduce.89.cloned.1.call-done = f32[256,256]{0,1:T(8,128)} async-done(((f32[256,256]{0,1:T(8,128)}), f32[256,256]{0,1:T(8,128)}) %all-reduce.89.cloned.1.call-update) | async-done | bytes 262160 | tf_op jit(solution)/shard_map/psum | solution.py:31
  5355.7 92.3 %all-reduce.91.cloned.1.call-done = f32[256,256]{0,1:T(8,128)} async-done(((f32[256,256]{0,1:T(8,128)}), f32[256,256]{0,1:T(8,128)}) %all-reduce.91.cloned.1.call-update) | async-done | bytes 262160 | tf_op jit(solution)/shard_map/psum | solution.py:29
  5732.0 92.1 %all-reduce.95.cloned.1.call-done = f32[256,256]{0,1:T(8,128)} async-done(((f32[256,256]{0,1:T(8,128)}), f32[256,256]{0,1:T(8,128)}) %all-reduce.95.cloned.1.call-update) | async-done | bytes 262160 | tf_op jit(solution)/shard_map/psum | solution.py:29
  5889.3 90.2 %all-reduce.97.cloned.1.call-done = f32[256,256]{0,1:T(8,128)} async-done(((f32[256,256]{0,1:T(8,128)}), f32[256,256]{0,1:T(8,128)}) %all-reduce.97.cloned.1.call-update) | async-done | bytes 262160 | tf_op jit(solution)/shard_map/psum | solution.py:31
  6108.4 91.7 %all-reduce.99.cloned.1.call-done = f32[256,256]{1,0:T(8,128)} async-done(((f32[256,256]{1,0:T(8,128)}), f32[256,256]{1,0:T(8,128)}) %all-reduce.99.cloned.1.call-update) | async-done | bytes 262160 | tf_op jit(solution)/shard_map/psum | solution.py:40
  (1101 shorter events, 4078.0 us)
Async XLA Ops:
  77.2 247.3 %all-reduce.37.cloned.1.call-start = ((), (), s32[]{:S(2)}) async-start(), calls=%async_computation.19 | async-start | bytes 524288 | tf_op jit(solution)/shard_map/psum | solution.py:31
  234.3 226.5 %reduce-scatter.20.cloned.1.call-start = ((), (), s32[]{:S(2)}) async-start(), calls=%async_computation.20 | async-start | bytes 1966080 | tf_op jit(solution)/shard_map/reduce_scatter | solution.py:25
  463.4 247.8 %all-reduce.41.cloned.1.call-start = ((), (), s32[]{:S(2)}) async-start(), calls=%async_computation.22 | async-start | bytes 524288 | tf_op jit(solution)/shard_map/psum | solution.py:31
  621.0 216.1 %reduce-scatter.22.cloned.1.call-start = ((), (), s32[]{:S(2)}) async-start(), calls=%async_computation.23 | async-start | bytes 1966080 | tf_op jit(solution)/shard_map/reduce_scatter | solution.py:25
  839.7 247.9 %all-reduce.45.cloned.1.call-start = ((), (), s32[]{:S(2)}) async-start(), calls=%async_computation.25 | async-start | bytes 524288 | tf_op jit(solution)/shard_map/psum | solution.py:31
  1216.1 247.8 %all-reduce.49.cloned.1.call-start = ((), (), s32[]{:S(2)}) async-start(), calls=%async_computation.28 | async-start | bytes 524288 | tf_op jit(solution)/shard_map/psum | solution.py:31
  1373.7 216.1 %reduce-scatter.26.cloned.1.call-start = ((), (), s32[]{:S(2)}) async-start(), calls=%async_computation.29 | async-start | bytes 1966080 | tf_op jit(solution)/shard_map/reduce_scatter | solution.py:25
  1592.4 247.8 %all-reduce.53.cloned.1.call-start = ((), (), s32[]{:S(2)}) async-start(), calls=%async_computation.31 | async-start | bytes 524288 | tf_op jit(solution)/shard_map/psum | solution.py:31
  1750.0 216.1 %reduce-scatter.28.cloned.1.call-start = ((), (), s32[]{:S(2)}) async-start(), calls=%async_computation.32 | async-start | bytes 1966080 | tf_op jit(solution)/shard_map/reduce_scatter | solution.py:25
  1968.7 247.7 %all-reduce.57.cloned.1.call-start = ((), (), s32[]{:S(2)}) async-start(), calls=%async_computation.34 | async-start | bytes 524288 | tf_op jit(solution)/shard_map/psum | solution.py:31
  2344.9 247.7 %all-reduce.61.cloned.1.call-start = ((), (), s32[]{:S(2)}) async-start(), calls=%async_computation.37 | async-start | bytes 524288 | tf_op jit(solution)/shard_map/psum | solution.py:31
  2502.4 216.1 %reduce-scatter.32.cloned.1.call-start = ((), (), s32[]{:S(2)}) async-start(), calls=%async_computation.38 | async-start | bytes 1966080 | tf_op jit(solution)/shard_map/reduce_scatter | solution.py:25
  2721.1 247.9 %all-reduce.65.cloned.1.call-start = ((), (), s32[]{:S(2)}) async-start(), calls=%async_computation.40 | async-start | bytes 524288 | tf_op jit(solution)/shard_map/psum | solution.py:31
  3097.4 247.8 %all-reduce.69.cloned.1.call-start = ((), (), s32[]{:S(2)}) async-start(), calls=%async_computation.43 | async-start | bytes 524288 | tf_op jit(solution)/shard_map/psum | solution.py:31
  3473.8 247.8 %all-reduce.73.cloned.1.call-start = ((), (), s32[]{:S(2)}) async-start(), calls=%async_computation.46 | async-start | bytes 524288 | tf_op jit(solution)/shard_map/psum | solution.py:31
  3631.4 216.1 %reduce-scatter.38.cloned.1.call-start = ((), (), s32[]{:S(2)}) async-start(), calls=%async_computation.47 | async-start | bytes 1966080 | tf_op jit(solution)/shard_map/reduce_scatter | solution.py:25
  3850.0 247.9 %all-reduce.77.cloned.1.call-start = ((), (), s32[]{:S(2)}) async-start(), calls=%async_computation.49 | async-start | bytes 524288 | tf_op jit(solution)/shard_map/psum | solution.py:31
  4226.6 247.8 %all-reduce.81.cloned.1.call-start = ((), (), s32[]{:S(2)}) async-start(), calls=%async_computation.52 | async-start | bytes 524288 | tf_op jit(solution)/shard_map/psum | solution.py:31
  4384.2 216.1 %reduce-scatter.42.cloned.1.call-start = ((), (), s32[]{:S(2)}) async-start(), calls=%async_computation.53 | async-start | bytes 1966080 | tf_op jit(solution)/shard_map/reduce_scatter | solution.py:25
  4602.9 247.8 %all-reduce.85.cloned.1.call-start = ((), (), s32[]{:S(2)}) async-start(), calls=%async_computation.55 | async-start | bytes 524288 | tf_op jit(solution)/shard_map/psum | solution.py:31
  4979.2 247.9 %all-reduce.89.cloned.1.call-start = ((), (), s32[]{:S(2)}) async-start(), calls=%async_computation.58 | async-start | bytes 524288 | tf_op jit(solution)/shard_map/psum | solution.py:31
  5136.9 216.1 %reduce-scatter.46.cloned.1.call-start = ((), (), s32[]{:S(2)}) async-start(), calls=%async_computation.59 | async-start | bytes 1966080 | tf_op jit(solution)/shard_map/reduce_scatter | solution.py:25
  5355.6 247.8 %all-reduce.93.cloned.1.call-start = ((), (), s32[]{:S(2)}) async-start(), calls=%async_computation.61 | async-start | bytes 524288 | tf_op jit(solution)/shard_map/psum | solution.py:31
  5732.0 247.5 %all-reduce.97.cloned.1.call-start = ((), (), s32[]{:S(2)}) async-start(), calls=%async_computation.64 | async-start | bytes 524288 | tf_op jit(solution)/shard_map/psum | solution.py:31
  (45 other events, 3918.5 us)
Sparse Core Ops, SparseCore 0:
  78.5 90.9 all-reduce.34
  234.5 90.0 all-reduce.36
  464.7 90.9 all-reduce.38
  841.1 91.0 all-reduce.42
  1217.5 90.9 all-reduce.46
  1593.7 90.9 all-reduce.50
  1750.1 90.0 all-reduce.52
  1969.9 91.0 all-reduce.54
  2346.1 90.9 all-reduce.58
  2722.5 90.9 all-reduce.62
  2878.9 90.0 all-reduce.64
  3098.7 90.9 all-reduce.66
  3475.0 91.0 all-reduce.70
  3631.5 90.0 all-reduce.72
  3851.5 91.0 all-reduce.74
  4227.8 91.0 all-reduce.78
  4384.3 90.0 all-reduce.80
  4604.2 90.9 all-reduce.82
  4980.5 91.0 all-reduce.86
  5137.0 90.0 all-reduce.88
  5356.9 90.9 all-reduce.90
  5733.1 90.9 all-reduce.94
  5889.3 90.0 all-reduce.96
  6109.1 90.9 all-reduce.98
  (26 shorter events, 1263.8 us)
where the time goes:
time: 6220 us; the launch traced here: 6210 us
  waiting for transfers between devices  3470 us (56%)
  other arithmetic  1800 us (29%)
  blocking collectives  507 us (8%)
  matrix products  171 us (3%)
  local copies, waits for them, and re-layouts  169 us (3%)
    psum x16, waiting for transfers between devices, orthonormalize(): lax.psum(jnp.einsum('ka,kb->ab', y_low, y_low, preferred_element_type=jnp...  1480 us
    psum x16, waiting for transfers between devices, orthonormalize(): lax.psum(jnp.einsum('ka,kb->ab', y_local, y_local, precision=HIGHEST, pre...  1440 us
    another operation x223, other arithmetic, cholesky_solve(): lower = jnp.linalg.cholesky(gram)  1110 us
    another operation x66, other arithmetic, cholesky_solve(): lax.linalg.triangular_solve(lower, block, left_side=False, lower=True, tr...  631 us
    all_gather x17, blocking collectives, apply_block(): x_column = lax.all_gather(x_moved, 'row', axis=0, tiled=True)  507 us
    reduce_scatter x17, waiting for transfers between devices, apply_block(): return lax.psum_scatter(part_sum, 'col', scatter_dimension=0, tiled=True)  456 us
    another operation x225, local copies, waits for them, and re-layouts, cholesky_solve(): lax.linalg.triangular_solve(lower, block, left_side=False, lower=True, tr...  130 us
  transfers between devices with their start and end apart: 67, of which 50 were waited for; matrix products, arithmetic and copies ran while one was open for 0% of the time, Pallas kernels for 0%

commit v1 on v0

v1 whole, which is shorter than its diff:
```python
import functools
import jax, jax.numpy as jnp
from jax import lax
from jax.experimental import pallas as pl
from jax.experimental.pallas import tpu as pltpu
HIGHEST = lax.Precision.HIGHEST
N = 256; NB = 16; LANES = 128

def dot(a, b, dims=((1,), (0,))):
    return lax.dot_general(a, b, (dims, ((), ())), precision=HIGHEST, preferred_element_type=jnp.float32)

def inverse_factor(w, out, qpad):
    rows = lax.broadcasted_iota(jnp.int32, (NB, LANES), 0)
    lanes = lax.broadcasted_iota(jnp.int32, (NB, LANES), 1)
    qpad[...] = jnp.zeros_like(qpad)
    for k in range(0, N, NB):
        grp, off = k // LANES, k % LANES
        panel = [w[k:k+NB, g*LANES:(g+1)*LANES] for g in range(2)]
        cols = [jnp.broadcast_to(panel[grp][:, off+m:off+m+1], (NB, LANES)) for m in range(NB)]
        for j in range(NB):
            here = rows == j
            pivot = cols[j][j:j+1, :]
            inv = 1.0 / pivot
            root = lax.rsqrt(pivot)
            panel[grp] = jnp.where(lanes == off + j, here.astype(jnp.float32), panel[grp])
            coef = cols[j]
            for g in range(2):
                row = panel[g][j:j+1, :]
                out[k+j:k+j+1, g*LANES:(g+1)*LANES] = jnp.where(
                    lax.broadcasted_iota(jnp.int32, (1, LANES), 1) + g*LANES <= k + j, row * root, 0.0)
                q = row * inv
                panel[g] = jnp.where(here, q, panel[g] - coef * q)
            for m in range(j+1, NB):
                q = cols[m][j:j+1, :] * inv
                cols[m] = jnp.where(here, q, cols[m] - coef * q)
        if k + NB < N:
            if off >= NB:
                qpad[off-NB:off, :] = jnp.zeros((NB, N), jnp.float32)
            elif k:
                qpad[LANES-NB:LANES, :] = jnp.zeros((NB, N), jnp.float32)
            for g in range(2):
                qpad[off:off+NB, g*LANES:(g+1)*LANES] = panel[g]
            q = qpad[...]
            pieces = [(k+NB, k+2*NB)]
            if k + 2*NB < N:
                pieces.append((k+2*NB, N))
            for lo, hi in pieces:
                lhs = w[lo:hi, grp*LANES:(grp+1)*LANES]
                t = dot(lhs, q)
                lane = lax.broadcasted_iota(jnp.int32, (hi-lo, N), 1)
                old = w[lo:hi, :]
                w[lo:hi, :] = jnp.where((lane >= k) & (lane < k+NB), 0.0, old) - t

def kernel(g1, s, y, x, w, inv1, inv2, qpad):
    w[...] = g1[...]
    inverse_factor(w, inv1, qpad)
    a = inv1[...]
    w[...] = dot(dot(a, s[...]), a, ((1,), (1,)))
    inverse_factor(w, inv2, qpad)
    n = dot(inv2[...], a)
    x[...] = dot(y[...], n, ((1,), (1,)))

def solve(g1, s, y):
    v = pltpu.VMEM
    return pl.pallas_call(kernel, out_shape=jax.ShapeDtypeStruct(y.shape, jnp.float32),
        in_specs=[pl.BlockSpec(memory_space=pltpu.VMEM)]*3, out_specs=pl.BlockSpec(memory_space=pltpu.VMEM),
        scratch_shapes=[v((N,N),jnp.float32)]*3+[v((LANES,N),jnp.float32)], name="solve")(g1, s, y)


def solution(mesh):
    from jax.sharding import PartitionSpec as P
    grid = ("row", "col")
    row_count, col_count = mesh.shape["row"], mesh.shape["col"]
    moves = [(i, (i % row_count) * col_count + i // row_count) for i in range(row_count * col_count)]

    def apply_block(op_block, x_local):
        x_moved = lax.ppermute(x_local.astype(jnp.bfloat16), grid, moves)
        x_column = lax.all_gather(x_moved, "row", axis=0, tiled=True)
        part_sum = jnp.dot(op_block, x_column, preferred_element_type=jnp.float32)
        return lax.psum_scatter(part_sum, "col", scatter_dimension=0, tiled=True)

    def local_program(op_block, x_local, shift_vals):
        def sweep(step, x_local):
            y_local = apply_block(op_block, x_local) - shift_vals[step] * x_local
            y_low = y_local.astype(jnp.bfloat16)
            gram_one = jnp.einsum("ka,kb->ab", y_low, y_low, preferred_element_type=jnp.float32)
            gram_full = jnp.einsum("ka,kb->ab", y_local, y_local, precision=HIGHEST, preferred_element_type=jnp.float32)
            grams = lax.psum(jnp.stack([gram_one, gram_full]), grid)
            return solve(grams[0], grams[1], y_local)
        x_local = lax.fori_loop(0, shift_vals.shape[0], sweep, x_local)
        image = apply_block(op_block, x_local)
        local_gram = jnp.einsum("ka,kb->ab", x_local, image, precision=HIGHEST, preferred_element_type=jnp.float32)
        return x_local, lax.psum(local_gram, grid)

    return jax.shard_map(
        local_program, mesh=mesh,
        in_specs=(P(("batch", "row"), "col"), P(("batch", "row", "col"), None), P("batch")),
        out_specs=(P(("batch", "row", "col"), None), P("batch", None)),
        check_vma=False,
    )
```

time: 6220 us -> 3010 us (0.48)
  other arithmetic: 1800 us -> 40.7 us
  waiting for transfers between devices: 3470 us -> 2010 us
  Pallas kernels: 0 us -> 272 us
  local copies, waits for them, and re-layouts: 169 us -> 41.8 us
  matrix products: 171 us -> 103 us
    another operation x289 -> x16, other arithmetic: 1740 us -> 13.2 us  [sweep(): grams = lax.psum(jnp.stack([gram_one, gram_full]), grid)]
    psum x33 -> x17, waiting for transfers between devices: 3010 us -> 1560 us  [the longest x16 1470 us: sweep(): grams = lax.psum(jnp.stack([gram_one, gram_full]), grid)]
    pallas_call x0 -> x16, Pallas kernels: none -> 272 us  [solve(): pl.pallas_call(kernel, out_shape=jax.ShapeDtypeStruct(y.shape, jnp.float3...]
    another operation x289 -> x0, local copies, waits for them, and re-layouts: 131 us -> none  [the longest x225 130 us: cholesky_solve(): lax.linalg.triangular_solve(lower, block, left_side=False, lower=True, tr...]
  transfers between devices with their start and end apart: 67 -> 51, of which waited for: 50 -> 34; matrix products, arithmetic and copies ran while one was open for 0% -> 0% of each run, Pallas kernels for 0% -> 0%
where the time goes in v1:
time: 3010 us
  waiting for transfers between devices  2010 us (67%)
  blocking collectives  506 us (17%)
  Pallas kernels  272 us (9%)
  matrix products  103 us (3%)
  local copies, waits for them, and re-layouts  41.8 us (1%)
  other arithmetic  40.7 us (1%)
    psum x16, waiting for transfers between devices, sweep(): grams = lax.psum(jnp.stack([gram_one, gram_full]), grid)  1470 us
    all_gather x17, blocking collectives, apply_block(): x_column = lax.all_gather(x_moved, 'row', axis=0, tiled=True)  506 us
    reduce_scatter x17, waiting for transfers between devices, apply_block(): return lax.psum_scatter(part_sum, 'col', scatter_dimension=0, tiled=True)  447 us
    pallas_call x16, Pallas kernels, solve(): pl.pallas_call(kernel, out_shape=jax.ShapeDtypeStruct(y.shape, jnp.float3...  272 us
    psum x1, waiting for transfers between devices, local_program(): return (x_local, lax.psum(local_gram, grid))  92.3 us
    dot_general x17, matrix products, apply_block(): part_sum = jnp.dot(op_block, x_column, preferred_element_type=jnp.float32)  83.1 us
  transfers between devices with their start and end apart: 51, of which 34 were waited for; matrix products, arithmetic and copies ran while one was open for 0% of the time, Pallas kernels for 0%

profile of v1, /device:TPU:0, one launch (start us, length us, event | category | flops | bytes accessed | tf_op | source)
XLA Modules:
  0.0 3005.5 jit_solution(1482601203436665522)
XLA Ops:
  9.0 2830.8 %while.13 = (s32[]{:T(128)}, f32[384,256]{1,0:T(8,128)S(1)}, bf16[1536,1536]{1,0:T(8,128)(2,1)}, f32[16]{0:T(128)}, s32[]{:T(128)}) while((s32[]{:T(128)}, f32[384,256]{1,0:T(8,128)S(1)}, bf16[1536,1536]{1,0:T(8,128)(2,1)}, f32[16]{0:T(128)}, s32[]{:T(128)}) %tuple.35), condition=%wide.region_3.0_spmd, body=%wide.region_0.0_spmd.sunk | while | flops 1560936448 | bytes 24642044 | solution.py:90
  9.7 31.4 %all_gather.12 = bf16[1536,256]{1,0:T(8,128)(2,1)S(1)} all-gather(bf16[384,256]{1,0:T(8,128)(2,1)S(1)} %collective-permute-done), channel_id=1, replica_groups=mesh['batch'=2,'row'=4,'col'=4] {'row'}, dimensions={0}, use_global_device_ids=true | all-gather | bytes 983040 | tf_op jit(solution)/shard_map/while/body/eval_jaxpr/all_gather | solution.py:78
  78.9 92.0 %all-reduce.5.cloned.1.call-done = f32[2,256,256]{2,1,0:T(8,128)} async-done(((f32[2,256,256]{2,1,0:T(8,128)}), f32[2,256,256]{2,1,0:T(8,128)}) %all-reduce.5.cloned.1.call-update) | async-done | bytes 524304 | tf_op jit(solution)/shard_map/while/body/eval_jaxpr/psum | solution.py:88
  190.6 29.7 all_gather.12
  255.6 92.0 %all-reduce.5.cloned.1.call-done = f32[2,256,256]{2,1,0:T(8,128)} async-done(((f32[2,256,256]{2,1,0:T(8,128)}), f32[2,256,256]{2,1,0:T(8,128)}) %all-reduce.5.cloned.1.call-update) | async-done | bytes 524304 | tf_op jit(solution)/shard_map/while/body/eval_jaxpr/psum | solution.py:88
  367.3 29.7 all_gather.12
  432.3 92.0 %all-reduce.5.cloned.1.call-done = f32[2,256,256]{2,1,0:T(8,128)} async-done(((f32[2,256,256]{2,1,0:T(8,128)}), f32[2,256,256]{2,1,0:T(8,128)}) %all-reduce.5.cloned.1.call-update) | async-done | bytes 524304 | tf_op jit(solution)/shard_map/while/body/eval_jaxpr/psum | solution.py:88
  608.9 91.9 %all-reduce.5.cloned.1.call-done = f32[2,256,256]{2,1,0:T(8,128)} async-done(((f32[2,256,256]{2,1,0:T(8,128)}), f32[2,256,256]{2,1,0:T(8,128)}) %all-reduce.5.cloned.1.call-update) | async-done | bytes 524304 | tf_op jit(solution)/shard_map/while/body/eval_jaxpr/psum | solution.py:88
  720.5 29.7 all_gather.12
  785.6 92.0 %all-reduce.5.cloned.1.call-done = f32[2,256,256]{2,1,0:T(8,128)} async-done(((f32[2,256,256]{2,1,0:T(8,128)}), f32[2,256,256]{2,1,0:T(8,128)}) %all-reduce.5.cloned.1.call-update) | async-done | bytes 524304 | tf_op jit(solution)/shard_map/while/body/eval_jaxpr/psum | solution.py:88
  962.2 92.0 %all-reduce.5.cloned.1.call-done = f32[2,256,256]{2,1,0:T(8,128)} async-done(((f32[2,256,256]{2,1,0:T(8,128)}), f32[2,256,256]{2,1,0:T(8,128)}) %all-reduce.5.cloned.1.call-update) | async-done | bytes 524304 | tf_op jit(solution)/shard_map/while/body/eval_jaxpr/psum | solution.py:88
  1073.8 29.7 all_gather.12
  1138.9 92.0 %all-reduce.5.cloned.1.call-done = f32[2,256,256]{2,1,0:T(8,128)} async-done(((f32[2,256,256]{2,1,0:T(8,128)}), f32[2,256,256]{2,1,0:T(8,128)}) %all-reduce.5.cloned.1.call-update) | async-done | bytes 524304 | tf_op jit(solution)/shard_map/while/body/eval_jaxpr/psum | solution.py:88
  1315.5 92.0 %all-reduce.5.cloned.1.call-done = f32[2,256,256]{2,1,0:T(8,128)} async-done(((f32[2,256,256]{2,1,0:T(8,128)}), f32[2,256,256]{2,1,0:T(8,128)}) %all-reduce.5.cloned.1.call-update) | async-done | bytes 524304 | tf_op jit(solution)/shard_map/while/body/eval_jaxpr/psum | solution.py:88
  1492.2 92.0 %all-reduce.5.cloned.1.call-done = f32[2,256,256]{2,1,0:T(8,128)} async-done(((f32[2,256,256]{2,1,0:T(8,128)}), f32[2,256,256]{2,1,0:T(8,128)}) %all-reduce.5.cloned.1.call-update) | async-done | bytes 524304 | tf_op jit(solution)/shard_map/while/body/eval_jaxpr/psum | solution.py:88
  1603.8 29.7 all_gather.12
  1668.8 92.0 %all-reduce.5.cloned.1.call-done = f32[2,256,256]{2,1,0:T(8,128)} async-done(((f32[2,256,256]{2,1,0:T(8,128)}), f32[2,256,256]{2,1,0:T(8,128)}) %all-reduce.5.cloned.1.call-update) | async-done | bytes 524304 | tf_op jit(solution)/shard_map/while/body/eval_jaxpr/psum | solution.py:88
  1845.5 92.0 %all-reduce.5.cloned.1.call-done = f32[2,256,256]{2,1,0:T(8,128)} async-done(((f32[2,256,256]{2,1,0:T(8,128)}), f32[2,256,256]{2,1,0:T(8,128)}) %all-reduce.5.cloned.1.call-update) | async-done | bytes 524304 | tf_op jit(solution)/shard_map/while/body/eval_jaxpr/psum | solution.py:88
  2022.2 92.0 %all-reduce.5.cloned.1.call-done = f32[2,256,256]{2,1,0:T(8,128)} async-done(((f32[2,256,256]{2,1,0:T(8,128)}), f32[2,256,256]{2,1,0:T(8,128)}) %all-reduce.5.cloned.1.call-update) | async-done | bytes 524304 | tf_op jit(solution)/shard_map/while/body/eval_jaxpr/psum | solution.py:88
  2198.8 92.0 %all-reduce.5.cloned.1.call-done = f32[2,256,256]{2,1,0:T(8,128)} async-done(((f32[2,256,256]{2,1,0:T(8,128)}), f32[2,256,256]{2,1,0:T(8,128)}) %all-reduce.5.cloned.1.call-update) | async-done | bytes 524304 | tf_op jit(solution)/shard_map/while/body/eval_jaxpr/psum | solution.py:88
  2375.4 92.0 %all-reduce.5.cloned.1.call-done = f32[2,256,256]{2,1,0:T(8,128)} async-done(((f32[2,256,256]{2,1,0:T(8,128)}), f32[2,256,256]{2,1,0:T(8,128)}) %all-reduce.5.cloned.1.call-update) | async-done | bytes 524304 | tf_op jit(solution)/shard_map/while/body/eval_jaxpr/psum | solution.py:88
  2552.1 92.0 %all-reduce.5.cloned.1.call-done = f32[2,256,256]{2,1,0:T(8,128)} async-done(((f32[2,256,256]{2,1,0:T(8,128)}), f32[2,256,256]{2,1,0:T(8,128)}) %all-reduce.5.cloned.1.call-update) | async-done | bytes 524304 | tf_op jit(solution)/shard_map/while/body/eval_jaxpr/psum | solution.py:88
  2728.7 92.0 %all-reduce.5.cloned.1.call-done = f32[2,256,256]{2,1,0:T(8,128)} async-done(((f32[2,256,256]{2,1,0:T(8,128)}), f32[2,256,256]{2,1,0:T(8,128)}) %all-reduce.5.cloned.1.call-update) | async-done | bytes 524304 | tf_op jit(solution)/shard_map/while/body/eval_jaxpr/psum | solution.py:88
  2904.4 92.3 %all-reduce.3.cloned.1.call-done = f32[256,256]{1,0:T(8,128)} async-done(((f32[256,256]{1,0:T(8,128)}), f32[256,256]{1,0:T(8,128)}) %all-reduce.3.cloned.1.call-update) | async-done | bytes 262160 | tf_op jit(solution)/shard_map/psum | solution.py:93
  (345 shorter events, 1244.4 us)
Async XLA Ops:
  9.0 66.3 %reduce-scatter.5.cloned.1.call-start = ((), (), s32[]{:S(2)}) async-start(), calls=%async_computation.4 | async-start | bytes 1966080 | tf_op jit(solution)/shard_map/while/body/eval_jaxpr/reduce_scatter | solution.py:80
  46.0 124.9 %all-reduce.5.cloned.1.call-start = ((), (), s32[]{:S(2)}) async-start(), calls=%async_computation.5 | async-start | bytes 1048576 | tf_op jit(solution)/shard_map/while/body/eval_jaxpr/psum | solution.py:88
  225.1 122.5 %all-reduce.5.cloned.1.call-start = ((), (), s32[]{:S(2)}) async-start(), calls=%async_computation.5 | async-start | bytes 1048576 | tf_op jit(solution)/shard_map/while/body/eval_jaxpr/psum | solution.py:88
  366.5 62.2 %reduce-scatter.5.cloned.1.call-start = ((), (), s32[]{:S(2)}) async-start(), calls=%async_computation.4 | async-start | bytes 1966080 | tf_op jit(solution)/shard_map/while/body/eval_jaxpr/reduce_scatter | solution.py:80
  401.8 122.5 %all-reduce.5.cloned.1.call-start = ((), (), s32[]{:S(2)}) async-start(), calls=%async_computation.5 | async-start | bytes 1048576 | tf_op jit(solution)/shard_map/while/body/eval_jaxpr/psum | solution.py:88
  578.5 122.4 %all-reduce.5.cloned.1.call-start = ((), (), s32[]{:S(2)}) async-start(), calls=%async_computation.5 | async-start | bytes 1048576 | tf_op jit(solution)/shard_map/while/body/eval_jaxpr/psum | solution.py:88
  719.7 62.2 %reduce-scatter.5.cloned.1.call-start = ((), (), s32[]{:S(2)}) async-start(), calls=%async_computation.4 | async-start | bytes 1966080 | tf_op jit(solution)/shard_map/while/body/eval_jaxpr/reduce_scatter | solution.py:80
  755.1 122.5 %all-reduce.5.cloned.1.call-start = ((), (), s32[]{:S(2)}) async-start(), calls=%async_computation.5 | async-start | bytes 1048576 | tf_op jit(solution)/shard_map/while/body/eval_jaxpr/psum | solution.py:88
  896.4 62.2 %reduce-scatter.5.cloned.1.call-start = ((), (), s32[]{:S(2)}) async-start(), calls=%async_computation.4 | async-start | bytes 1966080 | tf_op jit(solution)/shard_map/while/body/eval_jaxpr/reduce_scatter | solution.py:80
  931.8 122.4 %all-reduce.5.cloned.1.call-start = ((), (), s32[]{:S(2)}) async-start(), calls=%async_computation.5 | async-start | bytes 1048576 | tf_op jit(solution)/shard_map/while/body/eval_jaxpr/psum | solution.py:88
  1108.4 122.4 %all-reduce.5.cloned.1.call-start = ((), (), s32[]{:S(2)}) async-start(), calls=%async_computation.5 | async-start | bytes 1048576 | tf_op jit(solution)/shard_map/while/body/eval_jaxpr/psum | solution.py:88
  1285.1 122.5 %all-reduce.5.cloned.1.call-start = ((), (), s32[]{:S(2)}) async-start(), calls=%async_computation.5 | async-start | bytes 1048576 | tf_op jit(solution)/shard_map/while/body/eval_jaxpr/psum | solution.py:88
  1426.4 62.2 %reduce-scatter.5.cloned.1.call-start = ((), (), s32[]{:S(2)}) async-start(), calls=%async_computation.4 | async-start | bytes 1966080 | tf_op jit(solution)/shard_map/while/body/eval_jaxpr/reduce_scatter | solution.py:80
  1461.7 122.4 %all-reduce.5.cloned.1.call-start = ((), (), s32[]{:S(2)}) async-start(), calls=%async_computation.5 | async-start | bytes 1048576 | tf_op jit(solution)/shard_map/while/body/eval_jaxpr/psum | solution.py:88
  1638.4 122.4 %all-reduce.5.cloned.1.call-start = ((), (), s32[]{:S(2)}) async-start(), calls=%async_computation.5 | async-start | bytes 1048576 | tf_op jit(solution)/shard_map/while/body/eval_jaxpr/psum | solution.py:88
  1815.0 122.5 %all-reduce.5.cloned.1.call-start = ((), (), s32[]{:S(2)}) async-start(), calls=%async_computation.5 | async-start | bytes 1048576 | tf_op jit(solution)/shard_map/while/body/eval_jaxpr/psum | solution.py:88
  1956.3 62.2 %reduce-scatter.5.cloned.1.call-start = ((), (), s32[]{:S(2)}) async-start(), calls=%async_computation.4 | async-start | bytes 1966080 | tf_op jit(solution)/shard_map/while/body/eval_jaxpr/reduce_scatter | solution.py:80
  1991.7 122.4 %all-reduce.5.cloned.1.call-start = ((), (), s32[]{:S(2)}) async-start(), calls=%async_computation.5 | async-start | bytes 1048576 | tf_op jit(solution)/shard_map/while/body/eval_jaxpr/psum | solution.py:88
  2168.3 122.4 %all-reduce.5.cloned.1.call-start = ((), (), s32[]{:S(2)}) async-start(), calls=%async_computation.5 | async-start | bytes 1048576 | tf_op jit(solution)/shard_map/while/body/eval_jaxpr/psum | solution.py:88
  2345.0 122.5 %all-reduce.5.cloned.1.call-start = ((), (), s32[]{:S(2)}) async-start(), calls=%async_computation.5 | async-start | bytes 1048576 | tf_op jit(solution)/shard_map/while/body/eval_jaxpr/psum | solution.py:88
  2486.3 62.2 %reduce-scatter.5.cloned.1.call-start = ((), (), s32[]{:S(2)}) async-start(), calls=%async_computation.4 | async-start | bytes 1966080 | tf_op jit(solution)/shard_map/while/body/eval_jaxpr/reduce_scatter | solution.py:80
  2521.7 122.4 %all-reduce.5.cloned.1.call-start = ((), (), s32[]{:S(2)}) async-start(), calls=%async_computation.5 | async-start | bytes 1048576 | tf_op jit(solution)/shard_map/while/body/eval_jaxpr/psum | solution.py:88
  2698.3 122.4 %all-reduce.5.cloned.1.call-start = ((), (), s32[]{:S(2)}) async-start(), calls=%async_computation.5 | async-start | bytes 1048576 | tf_op jit(solution)/shard_map/while/body/eval_jaxpr/psum | solution.py:88
  2875.2 121.5 %all-reduce.3.cloned.1.call-start = ((), (), s32[]{:S(2)}) async-start(), calls=%async_computation.3 | async-start | bytes 524288 | tf_op jit(solution)/shard_map/psum | solution.py:93
  (60 other events, 2307.2 us)
Sparse Core Ops, SparseCore 0:
  46.1 29.1 reduce-scatter.4
  79.1 91.8 all-reduce.4
  255.7 91.8 all-reduce.4
  402.0 26.6 reduce-scatter.4
  432.4 91.8 all-reduce.4
  609.1 91.7 all-reduce.4
  755.2 26.6 reduce-scatter.4
  785.7 91.8 all-reduce.4
  931.9 26.6 reduce-scatter.4
  962.4 91.8 all-reduce.4
  1139.0 91.8 all-reduce.4
  1285.2 26.6 reduce-scatter.4
  1315.6 91.8 all-reduce.4
  1461.9 26.6 reduce-scatter.4
  1492.3 91.8 all-reduce.4
  1668.9 91.8 all-reduce.4
  1845.6 91.8 all-reduce.4
  1991.8 26.6 reduce-scatter.4
  2022.3 91.8 all-reduce.4
  2198.9 91.8 all-reduce.4
  2375.5 91.8 all-reduce.4
  2521.8 26.6 reduce-scatter.4
  2552.2 91.8 all-reduce.4
  2728.9 91.8 all-reduce.4
  (8 shorter events, 212.5 us)
Sparse Core Ops, SparseCore 1:
  2875.3 26.6 reduce-scatter.2
  2905.7 91.0 all-reduce.2

commit v2 on v0

v2 whole, which is shorter than its diff:
```python
import functools

import jax
import jax.numpy as jnp
from jax import lax
from jax.experimental import pallas as pl
from jax.experimental.pallas import tpu as pltpu
from jax.sharding import PartitionSpec as P

HIGHEST = lax.Precision.HIGHEST
MESH = pl.DeviceIdType.MESH
LANES = 128
STEP = 16


def dot(a, b, dims=((1,), (0,))):
    return lax.dot_general(a, b, (dims, ((), ())), precision=HIGHEST, preferred_element_type=jnp.float32)


def inverse_factor(w, out, qpad, hook=None):
    n = w.shape[0]
    groups = n // LANES
    shape = (groups, STEP, LANES)
    rows = lax.broadcasted_iota(jnp.int32, (STEP, LANES), 0)
    spot = lax.broadcasted_iota(jnp.int32, shape, 0) * LANES + lax.broadcasted_iota(jnp.int32, shape, 2)
    qpad[...] = jnp.zeros_like(qpad)
    for k in range(0, n, STEP):
        if hook is not None:
            hook(k)
        grp, off = k // LANES, k % LANES
        panel = jnp.stack([w[k:k + STEP, g * LANES:(g + 1) * LANES] for g in range(groups)])
        cols = jnp.stack([jnp.broadcast_to(panel[grp][:, off + m:off + m + 1], (STEP, LANES)) for m in range(STEP)])
        done = []
        for j in range(STEP):
            here = (rows == j)[None]
            coef = cols[0]
            pivot = coef[j:j + 1, :]
            inv = 1.0 / pivot
            panel = jnp.where(spot == k + j, here.astype(jnp.float32), panel)
            row = panel[:, j:j + 1, :]
            done.append(row * lax.rsqrt(pivot))
            q = row * inv
            panel = jnp.where(here, q, panel - coef * q)
            if j + 1 < STEP:
                q = cols[1:, j:j + 1, :] * inv
                cols = jnp.where(here, q, cols[1:] - coef * q)
        done = jnp.concatenate(done, axis=1)
        low = k + lax.broadcasted_iota(jnp.int32, shape, 1)
        done = jnp.where(spot <= low, done, 0.0)
        for g in range(groups):
            out[k:k + STEP, g * LANES:(g + 1) * LANES] = done[g]
        if k + STEP == n:
            break
        if k:
            last = (k - STEP) % LANES
            qpad[last:last + STEP, :] = jnp.zeros((STEP, n), jnp.float32)
        for g in range(groups):
            qpad[off:off + STEP, g * LANES:(g + 1) * LANES] = panel[g]
        q = qpad[...]
        pieces = [(k + STEP, k + 2 * STEP)] + ([(k + 2 * STEP, n)] if k + 2 * STEP < n else [])
        for lo, hi in pieces:
            t = dot(w[lo:hi, grp * LANES:(grp + 1) * LANES], q)
            lane = lax.broadcasted_iota(jnp.int32, (hi - lo, n), 1)
            w[lo:hi, :] = jnp.where((lane >= k) & (lane < k + STEP), 0.0, w[lo:hi, :]) - t


class GroupSum:
    def __init__(self, part, bufs, sems, z, c):
        self.part, self.z, self.c = part, z, c
        self.one, self.two, self.out = bufs
        self.send, self.recv = sems

    def _copies(self, phase):
        me = self.z if phase == 1 else self.c
        for i in range(1, 4):
            peer = lax.rem(me + i, 4)
            src = (self.part.at[peer], self.two.at[me], self.out.at[me])[phase]
            dst = (self.one, self.two, self.out)[phase].at[me]
            yield pltpu.make_async_remote_copy(
                src_ref=src, dst_ref=dst, send_sem=self.send.at[phase, i], recv_sem=self.recv.at[phase, me],
                device_id={"row": peer} if phase == 1 else {"col": peer}, device_id_type=MESH)

    def _start(self, phase):
        for copy in self._copies(phase):
            copy.start()

    def _finish(self, phase):
        me = self.z if phase == 1 else self.c
        land = (self.one, self.two, self.out)[phase]
        for i in range(1, 4):
            src = lax.rem(me + i, 4)
            pltpu.make_async_copy(land.at[src], land.at[src], self.recv.at[phase, src]).wait()
        for copy in self._copies(phase):
            copy.wait_send()

    def begin(self):
        self._start(0)

    def middle(self):
        self._finish(0)
        self.one[self.c] = self.part[self.c]
        self.two[self.z] = (self.one[0] + self.one[1]) + (self.one[2] + self.one[3])
        self._start(1)

    def last(self):
        self._finish(1)
        self.out[self.c] = (self.two[0] + self.two[1]) + (self.two[2] + self.two[3])
        self._start(2)

    def end(self):
        self._finish(2)


def symmetric(ref):
    flat = ref[...].reshape(3 * LANES, LANES)
    a, b, c = flat[:LANES], flat[LANES:2 * LANES], flat[2 * LANES:]
    return a, b, b.T, c


def kernel(sweeps, a_hbm, x0, sigma, x_out, h_out, arows, xg, acc, xs, ys, w, inv1, inv2, qpad, full,
           part1, part2, part3, b11, b12, b13, b21, b22, b23, b31, b32, b33,
           asend, arecv, aown, up, down, zrecv, ysend, yrecv, dsend, drecv,
           s1, r1, s2, r2, s3, r3):
    z, c = lax.axis_index("row"), lax.axis_index("col")
    y, k = c // 2, lax.rem(c, 2)
    rb, bc = x0.shape
    half = rb // 2
    width = a_hbm.shape[1]
    twin = c + 1 - 2 * k
    across = lax.rem(c + 2, 4)

    barrier = pltpu.get_barrier_semaphore()
    for i in range(1, 4):
        pl.semaphore_signal(barrier, inc=1, device_id={"col": lax.rem(c + i, 4)}, device_id_type=MESH)
        pl.semaphore_signal(barrier, inc=1, device_id={"row": lax.rem(z + i, 4)}, device_id_type=MESH)
    pl.semaphore_wait(barrier, 6)

    def columns(block):
        return pl.ds(pl.multiple_of(block * width, LANES), width)

    def spread(i):
        peer = lax.rem(c + i, 4)
        return pltpu.make_async_remote_copy(
            src_ref=a_hbm.at[pl.ds(pl.multiple_of(peer * rb, STEP), rb)], dst_ref=arows.at[:, columns(c)],
            send_sem=asend.at[i], recv_sem=arecv.at[c], device_id={"col": peer}, device_id_type=MESH)

    own_rows = pltpu.make_async_copy(a_hbm.at[pl.ds(pl.multiple_of(c * rb, STEP), rb)], arows.at[:, columns(c)], aown)
    for i in range(1, 4):
        spread(i).start()
    own_rows.start()
    xs[...] = x0[...]
    own_rows.wait()
    for i in range(1, 4):
        src = lax.rem(c + i, 4)
        land = arows.at[:, columns(src)]
        pltpu.make_async_copy(land, land, arecv.at[src]).wait()
    for i in range(1, 4):
        spread(i).wait_send()

    def sweep(t, carry):
        p = lax.rem(t, 2)

        def shard(yy, zz, kk):
            return xg.at[p, zz * 4 + yy * 2 + kk]

        def piece(yy, zz, kk, h):
            return xg.at[p, zz * 4 + yy * 2 + kk, pl.ds(h * half, half)]

        def z_copy(zz, h, step):
            sems = up if step > 0 else down
            return pltpu.make_async_remote_copy(
                src_ref=piece(y, zz, k, h), dst_ref=piece(y, zz, k, h), send_sem=sems.at[zz, h],
                recv_sem=zrecv.at[zz, h], device_id={"row": z + step}, device_id_type=MESH)

        def y_copy(zz, h):
            return pltpu.make_async_remote_copy(
                src_ref=piece(y, zz, k, h), dst_ref=piece(y, zz, k, h), send_sem=ysend.at[zz, h],
                recv_sem=yrecv.at[zz, h], device_id={"col": across}, device_id_type=MESH)

        def d_copy(yy, zz):
            return pltpu.make_async_remote_copy(
                src_ref=shard(yy, zz, k), dst_ref=shard(yy, zz, k), send_sem=dsend.at[yy, zz],
                recv_sem=drecv.at[yy, zz], device_id={"col": twin}, device_id_type=MESH)

        def landed(ref, sem):
            pltpu.make_async_copy(ref, ref, sem).wait()

        def relay(act):
            for h in range(2):
                for step, ok in ((1, z < 3), (-1, z > 0)):
                    @pl.when(ok)
                    def _():
                        act(z_copy(z, h, step))
                act(y_copy(z, h))
            act(d_copy(y, z))
            for d in range(1, 4):
                for step, there, on in ((1, z >= d, z < 3), (-1, z + d <= 3, z > 0)):
                    @pl.when(there)
                    def _():
                        zz = z - step * d
                        for h in range(2):
                            if act is start:
                                landed(piece(y, zz, k, h), zrecv.at[zz, h])

                            @pl.when(on)
                            def _():
                                act(z_copy(zz, h, step))
                            act(y_copy(zz, h))
                        act(d_copy(y, zz))

        def start(copy):
            copy.start()

        def sent(copy):
            copy.wait_send()

        def near(i):
            return lax.rem(z // 2 + i // 2, 2) * 2 + lax.rem(lax.rem(z, 2) + lax.rem(i, 2), 2)

        def consume(yy, zz):
            block = zz * 4 + yy * 2
            cols = pl.ds(pl.multiple_of(block * rb, LANES), 2 * rb)
            acc[...] += jnp.dot(arows[:, cols], xg[p, pl.ds(block, 2)].reshape(2 * rb, bc), preferred_element_type=jnp.float32)

        xg[p, z * 4 + c] = xs[...].astype(jnp.bfloat16)
        relay(start)
        acc[...] = jnp.zeros_like(acc)

        def same_plane(i, carry):
            zz = near(i)
            landed(shard(y, zz, 1 - k), drecv.at[y, zz])
            consume(y, zz)
            return carry

        def other_plane(i, carry):
            zz = near(i)
            for h in range(2):
                landed(piece(1 - y, zz, k, h), yrecv.at[zz, h])
            d_copy(1 - y, zz).start()
            landed(shard(1 - y, zz, 1 - k), drecv.at[1 - y, zz])
            consume(1 - y, zz)
            return carry

        lax.fori_loop(0, 4, same_plane, 0)
        lax.fori_loop(0, 4, other_plane, 0)

        @pl.when(t < sweeps)
        def _():
            shift = sigma[lax.rem(t, sweeps)]
            yv = acc[...] - shift * xs[...]
            ys[...] = yv
            low = yv.astype(jnp.bfloat16)

            def lower(v, mul):
                v0, v1 = v[:, :LANES], v[:, LANES:]
                return [mul(a, b).reshape(LANES, LANES) for a, b in ((v0, v0), (v1, v0), (v1, v1))]

            def put(part, blocks):
                part[...] = jnp.concatenate(blocks, axis=0).reshape(part.shape)

            put(part1, lower(low, lambda a, b: lax.dot_general(a, b, (((0,), (0,)), ((), ())), preferred_element_type=jnp.float32)))
            one = GroupSum(part1, (b11, b12, b13), (s1, r1), z, c)
            one.begin()
            put(part2, lower(yv, lambda a, b: dot(a, b, ((0,), (0,)))))
            two = GroupSum(part2, (b21, b22, b23), (s2, r2), z, c)
            two.begin()
            one.middle()
            relay(sent)
            for zz in range(4):
                d_copy(1 - y, zz).wait_send()
            one.last()
            two.middle()
            one.end()

            def load(dst, ref):
                a, b, bt, d = symmetric(ref)
                dst[:LANES, :LANES] = a
                dst[LANES:, :LANES] = b
                dst[:LANES, LANES:] = bt
                dst[LANES:, LANES:] = d

            load(w, b13)

            def factor(turn, carry):
                def hook(col):
                    if col in (6 * STEP, 12 * STEP):
                        @pl.when(turn == 0)
                        def _():
                            if col == 6 * STEP:
                                two.last()
                            else:
                                two.end()
                                load(full, b23)

                inverse_factor(w, inv2, qpad, hook)

                @pl.when(turn == 0)
                def _():
                    first = inv2[...]
                    inv1[...] = first
                    w[...] = dot(dot(first, full[...]), first, ((1,), (1,)))
                return carry

            lax.fori_loop(0, 2, factor, 0)
            xs[...] = dot(ys[...], dot(inv2[...], inv1[...]), ((1,), (1,)))

        @pl.when(t == sweeps)
        def _():
            xv, zv = xs[...], acc[...]
            blocks = [dot(xv[:, i:i + LANES], zv[:, j:j + LANES], ((0,), (0,)))
                      for i in (0, LANES) for j in (0, LANES)]
            for i in range(4):
                part3[i] = blocks[i]
            three = GroupSum(part3, (b31, b32, b33), (s3, r3), z, c)
            three.begin()
            three.middle()
            relay(sent)
            for zz in range(4):
                d_copy(1 - y, zz).wait_send()
            three.last()
            three.end()
            for i in range(2):
                for j in range(2):
                    h_out[i * LANES:(i + 1) * LANES, j * LANES:(j + 1) * LANES] = b33[2 * i + j]
        return carry

    lax.fori_loop(0, sweeps + 1, sweep, 0)
    x_out[...] = xs[...]


def solution(mesh):
    if mesh.shape["row"] != 4 or mesh.shape["col"] != 4:
        raise ValueError("grid")

    def local_program(op_block, x_local, shift_vals):
        rb, bc = x_local.shape
        rows, width = op_block.shape
        f32, low = jnp.float32, jnp.bfloat16
        vmem, dma = pltpu.VMEM, pltpu.SemaphoreType.DMA
        piece, square = vmem((4, 96, LANES), f32), vmem((bc, bc), f32)
        wide = vmem((4, LANES, LANES), f32)
        return pl.pallas_call(
            functools.partial(kernel, shift_vals.shape[0]),
            out_shape=(jax.ShapeDtypeStruct((rb, bc), f32), jax.ShapeDtypeStruct((bc, bc), f32)),
            in_specs=[pl.BlockSpec(memory_space=pl.ANY), pl.BlockSpec(memory_space=pltpu.VMEM),
                      pl.BlockSpec(memory_space=pltpu.SMEM)],
            out_specs=(pl.BlockSpec(memory_space=pltpu.VMEM), pl.BlockSpec(memory_space=pltpu.VMEM)),
            scratch_shapes=[
                vmem((rb, 4 * width), low), vmem((2, 16, rb, bc), low), vmem((rb, bc), f32), vmem((rb, bc), f32),
                vmem((rb, bc), f32), square, square, square, vmem((LANES, bc), f32), square,
                piece, piece, wide, piece, piece, piece, piece, piece, piece, wide, wide, wide,
                dma((4,)), dma((4,)), dma, dma((4, 2)), dma((4, 2)), dma((4, 2)), dma((4, 2)), dma((4, 2)),
                dma((2, 4)), dma((2, 4)), dma((3, 4)), dma((3, 4)), dma((3, 4)), dma((3, 4)), dma((3, 4)), dma((3, 4)),
            ],
            compiler_params=pltpu.CompilerParams(collective_id=0, has_side_effects=True),
            name="subspace",
        )(op_block, x_local, shift_vals)

    return jax.shard_map(
        local_program, mesh=mesh,
        in_specs=(P(("batch", "row"), "col"), P(("batch", "row", "col"), None), P("batch")),
        out_specs=(P(("batch", "row", "col"), None), P("batch", None)),
        check_vma=False,
    )
```

time: 6220 us -> 990 us (0.16)
  waiting for transfers between devices: 3470 us -> 0 us
  other arithmetic: 1800 us -> 0 us
  Pallas kernels: 0 us -> 985 us
  blocking collectives: 507 us -> 0 us
  matrix products: 171 us -> 0 us
  local copies, waits for them, and re-layouts: 169 us -> 3.44 us
    psum x33 -> x0, waiting for transfers between devices: 3010 us -> none  [the longest x16 1480 us: orthonormalize(): lax.psum(jnp.einsum('ka,kb->ab', y_low, y_low, preferred_element_type=jnp...]
    another operation x289 -> x0, other arithmetic: 1740 us -> none  [the longest x223 1110 us: cholesky_solve(): lower = jnp.linalg.cholesky(gram)]
    pallas_call x0 -> x1, Pallas kernels: none -> 985 us  [local_program(): pl.pallas_call(functools.partial(kernel, shift_vals.shape[0]), out_shape=...]
    all_gather x17 -> x0, blocking collectives: 507 us -> none  [apply_block(): x_column = lax.all_gather(x_moved, 'row', axis=0, tiled=True)]
    reduce_scatter x17 -> x0, waiting for transfers between devices: 456 us -> none  [apply_block(): return lax.psum_scatter(part_sum, 'col', scatter_dimension=0, tiled=True)]
    another operation x289 -> x0, local copies, waits for them, and re-layouts: 131 us -> none  [the longest x225 130 us: cholesky_solve(): lax.linalg.triangular_solve(lower, block, left_side=False, lower=True, tr...]
    dot_general x50 -> x0, matrix products: 122 us -> none  [the longest x17 83.4 us: apply_block(): part_sum = jnp.dot(op_block, x_column, preferred_element_type=jnp.float32)]
  transfers between devices with their start and end apart: 67 -> 0, of which waited for: 50 -> 0; matrix products, arithmetic and copies ran while one was open for 0% -> 0% of each run, Pallas kernels for 0% -> 0%
where the time goes in v2:
time: 990 us; the launch traced here: 989 us
  Pallas kernels  985 us (99%)
    pallas_call x1, Pallas kernels, local_program(): pl.pallas_call(functools.partial(kernel, shift_vals.shape[0]), out_shape=...  985 us

profile of v2, /device:TPU:0, one launch (start us, length us, event | category | flops | bytes accessed | tf_op | source)
XLA Modules:
  0.0 989.3 jit_solution(16522366925895160961)
XLA Ops:
  0.6 985.2 %subspace.1 = (f32[384,256]{1,0:T(8,128)}, f32[256,256]{1,0:T(8,128)}) custom-call(bf16[1536,1536]{1,0:T(8,128)(2,1)} %a_hbm.1, f32[384,256]{1,0:T(8,128)} %x0.1, f32[16]{0:T(128)} %sigma.1), custom_call_target="tpu_custom_call" | custom-call | tf_op jit(solution)/shard_map/subspace/pallas_call | solution.py:342
  985.8 1.8 copy.7
  987.6 1.7 copy.8

commit v3 on v2

--- a/solution.py
+++ b/solution.py
@@ -11,6 +11,8 @@
 MESH = pl.DeviceIdType.MESH
 LANES = 128
 STEP = 16
+LIMIT = 1e-6
+GRID = ("row", "col")
 
 
 def dot(a, b, dims=((1,), (0,))):
@@ -64,6 +66,17 @@
             w[lo:hi, :] = jnp.where((lane >= k) & (lane < k + STEP), 0.0, w[lo:hi, :]) - t
 
 
+def refine(a, s):
+    n = a.shape[0]
+    i, j = lax.broadcasted_iota(jnp.int32, (n, n), 0), lax.broadcasted_iota(jnp.int32, (n, n), 1)
+    weight = jnp.where(i > j, 1.0, jnp.where(i == j, 0.5, 0.0))
+    eye = jnp.where(i == j, 1.0, 0.0)
+    one = weight * (dot(dot(a, s), a, ((1,), (1,))) - eye)
+    b = a - dot(one - dot(one, one), a)
+    two = weight * (dot(dot(b, s), b, ((1,), (1,))) - eye)
+    return b - dot(two, b), jnp.sum(jnp.sum(two * two, axis=0, keepdims=True), axis=1, keepdims=True)
+
+
 class GroupSum:
     def __init__(self, part, bufs, sems, z, c):
         self.part, self.z, self.c = part, z, c
@@ -117,10 +130,10 @@
     return a, b, b.T, c
 
 
-def kernel(sweeps, a_hbm, x0, sigma, x_out, h_out, arows, xg, acc, xs, ys, w, inv1, inv2, qpad, full,
+def kernel(sweeps, a_hbm, x0, sigma, x_out, h_out, bad_out, arows, xg, acc, xs, ys, w, inv1, qpad, full, worst, flags,
            part1, part2, part3, b11, b12, b13, b21, b22, b23, b31, b32, b33,
            asend, arecv, aown, up, down, zrecv, ysend, yrecv, dsend, drecv,
-           s1, r1, s2, r2, s3, r3):
+           s1, r1, s2, r2, s3, r3, fsend, frecv):
     z, c = lax.axis_index("row"), lax.axis_index("col")
     y, k = c // 2, lax.rem(c, 2)
     rb, bc = x0.shape
@@ -133,7 +146,9 @@
     for i in range(1, 4):
         pl.semaphore_signal(barrier, inc=1, device_id={"col": lax.rem(c + i, 4)}, device_id_type=MESH)
         pl.semaphore_signal(barrier, inc=1, device_id={"row": lax.rem(z + i, 4)}, device_id_type=MESH)
-    pl.semaphore_wait(barrier, 6)
+    other = 1 - lax.axis_index("batch")
+    pl.semaphore_signal(barrier, inc=1, device_id={"batch": other}, device_id_type=MESH)
+    pl.semaphore_wait(barrier, 7)
 
     def columns(block):
         return pl.ds(pl.multiple_of(block * width, LANES), width)
@@ -149,14 +164,7 @@
         spread(i).start()
     own_rows.start()
     xs[...] = x0[...]
-    own_rows.wait()
-    for i in range(1, 4):
-        src = lax.rem(c + i, 4)
-        land = arows.at[:, columns(src)]
-        pltpu.make_async_copy(land, land, arecv.at[src]).wait()
-    for i in range(1, 4):
-        spread(i).wait_send()
-
+    worst[...] = jnp.zeros_like(worst)
     def sweep(t, carry):
         p = lax.rem(t, 2)
 
@@ -226,6 +234,15 @@
         relay(start)
         acc[...] = jnp.zeros_like(acc)
 
+        @pl.when(t == 0)
+        def _():
+            own_rows.wait()
+            for i in range(1, 4):
+                src = lax.rem(c + i, 4)
+                landed(arows.at[:, columns(src)], arecv.at[src])
+            for i in range(1, 4):
+                spread(i).wait_send()
+
         def same_plane(i, carry):
             zz = near(i)
             landed(shard(y, zz, 1 - k), drecv.at[y, zz])
@@ -279,33 +296,26 @@
                 dst[:LANES, LANES:] = bt
                 dst[LANES:, LANES:] = d
 
+            def hook(col):
+                if col == 6 * STEP:
+                    two.last()
+                if col == 12 * STEP:
+                    two.end()
+                    load(full, b23)
+
             load(w, b13)
-
-            def factor(turn, carry):
-                def hook(col):
-                    if col in (6 * STEP, 12 * STEP):
-                        @pl.when(turn == 0)
-                        def _():
-                            if col == 6 * STEP:
-                                two.last()
-                            else:
-                                two.end()
-                                load(full, b23)
-
-                inverse_factor(w, inv2, qpad, hook)
-
-                @pl.when(turn == 0)
-                def _():
-                    first = inv2[...]
-                    inv1[...] = first
-                    w[...] = dot(dot(first, full[...]), first, ((1,), (1,)))
-                return carry
-
-            lax.fori_loop(0, 2, factor, 0)
-            xs[...] = dot(ys[...], dot(inv2[...], inv1[...]), ((1,), (1,)))
+            inverse_factor(w, inv1, qpad, hook)
+            inverse, left = refine(inv1[...], full[...])
+            xs[...] = dot(ys[...], inverse, ((1,), (1,)))
+            worst[...] = worst[...] + jnp.where(left <= LIMIT, 0.0, 1.0)
 
         @pl.when(t == sweeps)
         def _():
+            flags[1 - other] = worst[...]
+            tell = pltpu.make_async_remote_copy(
+                src_ref=flags.at[1 - other], dst_ref=flags.at[1 - other], send_sem=fsend, recv_sem=frecv,
+                device_id={"batch": other}, device_id_type=MESH)
+            tell.start()
             xv, zv = xs[...], acc[...]
             blocks = [dot(xv[:, i:i + LANES], zv[:, j:j + LANES], ((0,), (0,)))
                       for i in (0, LANES) for j in (0, LANES)]
@@ -319,6 +329,9 @@
                 d_copy(1 - y, zz).wait_send()
             three.last()
             three.end()
+            landed(flags.at[other], frecv)
+            tell.wait_send()
+            bad_out[...] = flags[0] + flags[1]
             for i in range(2):
                 for j in range(2):
                     h_out[i * LANES:(i + 1) * LANES, j * LANES:(j + 1) * LANES] = b33[2 * i + j]
@@ -326,6 +339,32 @@
 
     lax.fori_loop(0, sweeps + 1, sweep, 0)
     x_out[...] = xs[...]
+
+
+def plain_program(op_block, x_local, shift_vals):
+    moves = [(i, (i % 4) * 4 + i // 4) for i in range(16)]
+
+    def apply_block(x_local):
+        x_moved = lax.ppermute(x_local.astype(jnp.bfloat16), GRID, moves)
+        x_column = lax.all_gather(x_moved, "row", axis=0, tiled=True)
+        part_sum = jnp.dot(op_block, x_column, preferred_element_type=jnp.float32)
+        return lax.psum_scatter(part_sum, "col", scatter_dimension=0, tiled=True)
+
+    def orthonormalize(turn, y_local):
+        low = y_local.astype(jnp.bfloat16)
+        gram_one = jnp.einsum("ka,kb->ab", low, low, preferred_element_type=jnp.float32)
+        gram_two = jnp.einsum("ka,kb->ab", y_local, y_local, precision=HIGHEST, preferred_element_type=jnp.float32)
+        lower = jnp.linalg.cholesky(lax.psum(jnp.where(turn == 0, gram_one, gram_two), GRID))
+        return lax.linalg.triangular_solve(lower, y_local, left_side=False, lower=True, transpose_a=True)
+
+    def sweep(step, x_local):
+        y_local = apply_block(x_local) - shift_vals[step] * x_local
+        return lax.fori_loop(0, 2, orthonormalize, y_local)
+
+    x_local = lax.fori_loop(0, shift_vals.shape[0], sweep, x_local)
+    image = apply_block(x_local)
+    local_gram = jnp.einsum("ka,kb->ab", x_local, image, precision=HIGHEST, preferred_element_type=jnp.float32)
+    return x_local, lax.psum(local_gram, GRID)
 
 
 def solution(mesh):
@@ -339,22 +378,24 @@
         vmem, dma = pltpu.VMEM, pltpu.SemaphoreType.DMA
         piece, square = vmem((4, 96, LANES), f32), vmem((bc, bc), f32)
         wide = vmem((4, LANES, LANES), f32)
-        return pl.pallas_call(
+        x_fast, h_fast, bad = pl.pallas_call(
             functools.partial(kernel, shift_vals.shape[0]),
-            out_shape=(jax.ShapeDtypeStruct((rb, bc), f32), jax.ShapeDtypeStruct((bc, bc), f32)),
+            out_shape=(jax.ShapeDtypeStruct((rb, bc), f32), jax.ShapeDtypeStruct((bc, bc), f32),
+                       jax.ShapeDtypeStruct((8, LANES), f32)),
             in_specs=[pl.BlockSpec(memory_space=pl.ANY), pl.BlockSpec(memory_space=pltpu.VMEM),
                       pl.BlockSpec(memory_space=pltpu.SMEM)],
-            out_specs=(pl.BlockSpec(memory_space=pltpu.VMEM), pl.BlockSpec(memory_space=pltpu.VMEM)),
+            out_specs=(pl.BlockSpec(memory_space=pltpu.VMEM),) * 3,
             scratch_shapes=[
                 vmem((rb, 4 * width), low), vmem((2, 16, rb, bc), low), vmem((rb, bc), f32), vmem((rb, bc), f32),
-                vmem((rb, bc), f32), square, square, square, vmem((LANES, bc), f32), square,
+                vmem((rb, bc), f32), square, square, vmem((LANES, bc), f32), square, vmem((8, LANES), f32), vmem((2, 8, LANES), f32),
                 piece, piece, wide, piece, piece, piece, piece, piece, piece, wide, wide, wide,
                 dma((4,)), dma((4,)), dma, dma((4, 2)), dma((4, 2)), dma((4, 2)), dma((4, 2)), dma((4, 2)),
-                dma((2, 4)), dma((2, 4)), dma((3, 4)), dma((3, 4)), dma((3, 4)), dma((3, 4)), dma((3, 4)), dma((3, 4)),
+                dma((2, 4)), dma((2, 4)), dma((3, 4)), dma((3, 4)), dma((3, 4)), dma((3, 4)), dma((3, 4)), dma((3, 4)), dma, dma,
             ],
             compiler_params=pltpu.CompilerParams(collective_id=0, has_side_effects=True),
             name="subspace",
         )(op_block, x_local, shift_vals)
+        return lax.cond(bad[0, 0] == 0.0, lambda *args: (x_fast, h_fast), plain_program, op_block, x_local, shift_vals)
 
     return jax.shard_map(
         local_program, mesh=mesh,

time: 990 us -> 943 us (0.953)
  Pallas kernels: 985 us -> 923 us
  between operations: 0.64 us -> 14.7 us
    pallas_call x1, Pallas kernels: 985 us -> 923 us  [local_program(): pl.pallas_call(functools.partial(kernel, shift_vals.shape[0]), out_shape=...]
where the time goes in v3:
time: 943 us
  Pallas kernels  923 us (98%)
  between operations  14.7 us (2%)
    pallas_call x1, Pallas kernels, local_program(): pl.pallas_call(functools.partial(kernel, shift_vals.shape[0]), out_shape=...  923 us

profile of v3, /device:TPU:0, one launch (start us, length us, event | category | flops | bytes accessed | tf_op | source)
XLA Modules:
  0.0 942.6 jit_solution(5052219380608663229)
XLA Ops:
  7.2 0.0 copy-start
  7.2 0.0 copy-start.1
  7.2 923.4 %subspace.1 = (f32[384,256]{1,0:T(8,128)S(1)}, f32[256,256]{1,0:T(8,128)S(1)}, f32[8,128]{1,0:T(8,128)}) custom-call(bf16[1536,1536]{1,0:T(8,128)(2,1)} %a_hbm.1, f32[384,256]{1,0:T(8,128)} %x0.1, f32[16]{0:T(128)} %sigma.1), custom_call_target="tpu_custom_call" | custom-call | tf_op jit(solution)/shard_map/subspace/pallas_call | solution.py:381
  930.6 1.2 slice.87
  932.4 0.0 copy-done
  932.5 0.0 copy-done.1
  932.5 0.9 conditional.1
  932.7 0.7 copy.50
  933.4 0.7 copy.57
  934.1 1.7 copy.58
Async XLA Ops:
  7.2 925.3 %copy-start = (f32[384,256]{1,0:T(8,128)S(1)}, f32[384,256]{1,0:T(8,128)}, u32[]{:S(2)}) copy-start(f32[384,256]{1,0:T(8,128)} %x0.1) | copy-start | bytes 1179652
  7.2 925.3 %copy-start.1 = (f32[16]{0:T(128)S(1)}, f32[16]{0:T(128)}, u32[]{:S(2)}) copy-start(f32[16]{0:T(128)} %sigma.1) | copy-start | bytes 196
